TPU v7x, 128 devices: a whole 4x4x4 slice. The times are simulated.
128 devices in a mesh: band: 32 (over y, x, core), lev: 4 (over z).
Axes of the slice: x: 4, y: 4, z: 4, core: 2. Of those that a mesh axis runs over, the one named last changes fastest.
Arguments:
- increment: bfloat16 [32, 768, 1536], P('lev', 'band'), may hold values from -6 to 6
- background: float32 [384, 2, 32, 769], P(('band', 'lev')), may hold values from -6 to 6
- legendre: bfloat16 [384, 768, 769], P(('band', 'lev')), may hold values from -6 to 6, as said below
- coupling: float32 [4, 32, 32], replicated, may hold values from -1 to 1
- damping: float32 [4], replicated, may hold values from 0.5 to 4
- target_mass: float32 [1], replicated, may hold values from 1 to 4
- numerators: int32 [4], replicated, may hold values from 8 to 32
- pair_low: int32 [384], replicated, may hold values from 0 to 383, as said below
- lat_map: int32 [768], replicated, may hold values from 0 to 767, each once
Outputs:
- analysis: bfloat16 [32, 768, 1536], P('lev', 'band')
- corrections: float32 [4], replicated
Inputs may be any that keep to these rules, and one draw needn't show every extreme that they name: Slot p holds the wavenumbers pair_low[p] and 767 - pair_low[p]; every value appears once. For the slot p with pair_low[p] = 0, legendre[p, j, 0] = 1 at every latitude j. Stored grid row r lies on latitude lat_map[r]; every latitude appears once.
All inputs are finite; a program needn't handle non-finite values.
Results may differ from a plain program's by a relative error of at most 0.0078.
Values may be sent and summed in bfloat16 or wider, within the bound.
A program may use at most 128 MiB of HBM per device.

v0:
```python
import math

import jax
import jax.numpy as jnp
from jax import lax
from jax.sharding import Mesh
from jax.sharding import PartitionSpec as P

NT = 767
NLAT = 768
NLON = 1536
LEV = 32
STEPS = 4
DEN = 64
NPAIR = 384
BAND = ("band_0", "band_1", "band_2")
BAND_LEV = ("band_0", "band_1", "band_2", "lev")


def one_axis_at_a_time(array, axes):
    for axis in axes:
        array = lax.psum(array, axis)
    return array


def wave_table(pair_low):
    member = jnp.arange(4, dtype=jnp.int32) // 2
    re_im = jnp.arange(4, dtype=jnp.int32) % 2
    wavenumber = jnp.where(member[None, :] == 0, pair_low[:, None], NT - pair_low[:, None]).reshape(
        -1
    )
    part_of = jnp.tile(re_im, pair_low.shape[0])
    points = jnp.arange(NLON, dtype=jnp.int32)
    phase_idx = wavenumber[:, None] * points[None, :] % NLON
    angles = phase_idx.astype(jnp.float32) * (2.0 * math.pi / NLON)
    values = jnp.where(part_of[:, None] == 0, jnp.cos(angles), -jnp.sin(angles)) * math.sqrt(
        2.0 / NLON
    )
    return values.astype(jnp.bfloat16)


def lat_weights(lat_rows):
    return jnp.cos(math.pi * ((lat_rows.astype(jnp.float32) + 0.5) / NLAT - 0.5))


def degrees(low_wave):
    columns = jnp.arange(NT + 2, dtype=jnp.int32)
    in_second = columns[None, :] >= NT + 1 - low_wave[:, None]
    degree = jnp.where(in_second, columns[None, :] - 1, low_wave[:, None] + columns[None, :])
    return (degree.astype(jnp.float32), in_second)


def body(
    increment, background, legendre, coupling, damping, target_mass, numerators, pair_low, lat_map
):
    band_count = lax.axis_size(BAND)
    lev_count = lax.axis_size("lev")
    band_id = lax.axis_index(BAND)
    lev_id = lax.axis_index("lev")
    lev_dev = increment.shape[0]
    lat_dev = increment.shape[1]
    pair_dev = legendre.shape[0]
    fourier_tab = wave_table(pair_low)
    local_lats = lax.dynamic_slice_in_dim(lat_map, band_id * lat_dev, lat_dev)
    row_weight = lat_weights(local_lats)
    level_ids = (lev_id * lev_dev + jnp.arange(lev_dev, dtype=jnp.int32)).astype(jnp.float32)
    level_weight = 1.0 + 2.0 * level_ids / (LEV - 1)
    all_levels = 1.0 + 2.0 * jnp.arange(LEV, dtype=jnp.float32) / (LEV - 1)
    normaliser = (
        jnp.sum(all_levels) * jnp.sum(lat_weights(jnp.arange(NLAT, dtype=jnp.int32))) * NLON
    )
    fix_scale = math.sqrt(NT * NLON) / 2.0
    own_pairs = lax.dynamic_slice_in_dim(
        pair_low, (band_id * lev_count + lev_id) * pair_dev, pair_dev
    )
    degree, in_second = degrees(own_pairs)
    holder = (own_pairs == 0).astype(jnp.float32)
    stored = legendre[:, lat_map, :]
    fourier = jnp.einsum(
        "ck,xk->cx",
        fourier_tab,
        increment.reshape(lev_dev * lat_dev, NLON),
        preferred_element_type=jnp.float32,
    )
    fourier = (fourier.reshape(NPAIR, 4, lev_dev, lat_dev) * row_weight).astype(jnp.bfloat16)
    received = lax.all_to_all(fourier[None], BAND_LEV, split_axis=1, concat_axis=0, tiled=True)
    received = received.reshape(band_count, lev_count, pair_dev, 4, lev_dev, lat_dev)
    waves_in = received.transpose(2, 3, 1, 4, 0, 5).reshape(pair_dev, 4, LEV, NLAT)
    coeffs = jnp.einsum(
        "prj,pjc->prc",
        waves_in.reshape(pair_dev, 4 * LEV, NLAT),
        stored,
        preferred_element_type=jnp.float32,
    )
    coeffs = coeffs.reshape(pair_dev, 2, 2, LEV, NT + 2) * math.sqrt(2.0 / NLAT)
    second_cols = in_second[:, None, None, :]
    smoothing = 1.0 / (1.0 + (degree / NT) ** 4)
    incr_spec = jnp.where(second_cols, coeffs[:, 1], coeffs[:, 0]) * smoothing[:, None, None, :]
    shape_term = degree * (degree + 1.0) / (NT * (NT + 1.0))
    spectral = background
    fix_list = []
    grid_now = jnp.zeros((lev_dev, lat_dev, NLON), jnp.float32)
    for step_idx in range(STEPS):
        coupled = 0.7 * spectral + 0.4 * jnp.einsum(
            "lm,prmc->prlc", coupling[step_idx], spectral, precision=lax.Precision.HIGHEST
        )
        weight_now = numerators[step_idx].astype(jnp.float32) / DEN
        fresh = (
            coupled / (1.0 + damping[step_idx] * shape_term)[:, None, None, :]
            + weight_now * incr_spec
        )
        spectral = fresh
        spec_bf = spectral.astype(jnp.bfloat16)
        zeros_bf = jnp.zeros_like(spec_bf)
        split_rows = jnp.stack(
            [jnp.where(second_cols, zeros_bf, spec_bf), jnp.where(second_cols, spec_bf, zeros_bf)],
            axis=1,
        )
        waves_f = jnp.einsum(
            "prc,pjc->prj",
            split_rows.reshape(pair_dev, 4 * LEV, NT + 2),
            stored,
            preferred_element_type=jnp.float32,
        )
        waves_bf = (
            (waves_f * math.sqrt(2.0 / NT)).astype(jnp.bfloat16).reshape(pair_dev, 4, LEV, NLAT)
        )
        outgoing = waves_bf.reshape(pair_dev, 4, lev_count, lev_dev, band_count, lat_dev)
        outgoing = outgoing.transpose(4, 2, 0, 1, 3, 5).reshape(
            band_count * lev_count, pair_dev, 4, lev_dev, lat_dev
        )
        rows_back = lax.all_to_all(outgoing, BAND_LEV, split_axis=0, concat_axis=1, tiled=True)
        rows_back = rows_back.reshape(NPAIR * 4, lev_dev * lat_dev)
        grid_now = jnp.einsum(
            "cx,ck->xk", rows_back, fourier_tab, preferred_element_type=jnp.float32
        ).reshape(lev_dev, lat_dev, NLON)
        partial_value = jnp.sum(
            jnp.sum(jnp.exp(grid_now), axis=2) * level_weight[:, None] * row_weight[None, :]
        )
        total_mass = one_axis_at_a_time(partial_value, BAND_LEV) / normaliser
        mass_fix = jnp.log(target_mass[0] / total_mass)
        spectral = spectral.at[:, 0, :, 0].add(holder[:, None] * (mass_fix * fix_scale))
        fix_list.append(mass_fix)
    return (grid_now.astype(jnp.bfloat16), jnp.stack(fix_list))


def solution(mesh):
    finer = Mesh(
        mesh.devices.reshape(4, 4, 2, mesh.shape["lev"]), ("band_0", "band_1", "band_2", "lev")
    )
    placed = (
        P("lev", BAND, None),
        P(BAND_LEV, None, None, None),
        P(BAND_LEV, None, None),
        P(),
        P(),
        P(),
        P(),
        P(),
        P(),
    )
    return jax.shard_map(
        body, mesh=finer, in_specs=placed, out_specs=(P("lev", BAND, None), P()), check_vma=False
    )
```

profile of v0, /device:TPU:1, one launch (start us, length us, event | category | flops | bytes accessed | tf_op | source)
XLA Modules:
  0.0 629.1 jit_solution(11699386718393414058)
XLA Ops:
  3.2 40.4 %fusion.146 = bf16[384,4,1536,1]{2,0,3,1:T(8,128)(2,1)S(1)} fusion(s32[384,4]{0,1:T(4,128)S(1)} %copy.68, pred[4]{0:T(512)(128)(4,1)S(1)} %fusion.95), kind=kLoop, calls=%fused_computation.17.clone.clone.clone.clone.clone.clone.clone.clone.1 | loop fusion | flops 30670848 | bytes 4724740 | tf_op jit(solution)/shard_map/ck,xk->cx/dot_general | solution.py:79
  45.4 5.1 copy.69
  50.5 6.3 %reshape.556 = bf16[128,2,1152]{2,1,0:T(2,128)(2,1)} reshape(bf16[384,1,4,8,24]{4,3,2,1,0:T(8,128)(2,1)} %bitcast.214) | data formatting | bytes 1179648
  56.8 11.8 %all-to-all-start = ((bf16[128,2,1152]{2,1,0:T(2,128)(2,1)}), bf16[128,2,1152]{2,1,0:T(2,128)(2,1)S(1)}, u32[]{:S(2)}, u32[]{:S(2)}) async-start(bf16[128,2,1152]{2,1,0:T(2,128)(2,1)} %reshape.556), calls=%async_computation | async-start | bytes 1179648 | tf_op jit(solution)/shard_map/all_to_all | solution.py:86
  74.0 11.0 %copy.71 = bf16[3,768,769]{2,0,1:T(4,128)(2,1)} copy(bf16[3,768,769]{1,2,0:T(8,128)(2,1)} %param.17) | data formatting | bytes 7087104 | tf_op args[2]
  84.9 11.5 %gather_fusion = bf16[768,3,769]{2,1,0:T(4,128)(2,1)} fusion(bf16[3,768,769]{2,0,1:T(4,128)(2,1)} %copy.71, s32[1024]{0:T(1024)S(1)} %pad_clamp_fusion), kind=kCustom, calls=%fused_computation | custom fusion | bytes 7090176 | tf_op jit(solution)/shard_map/gather | solution.py:78
  96.5 9.8 %copy.72 = bf16[3,768,769]{1,2,0:T(8,128)(2,1)} copy(bf16[3,768,769]{2,0,1:T(4,128)(2,1)} %bitcast.213) | data formatting | bytes 7087104 | tf_op jit(solution)/shard_map/gather | solution.py:78
  106.5 5.7 reshape.557
  112.2 7.2 %copy.70 = bf16[3,4,4,8,32,24]{5,4,3,2,1,0:T(8,128)(2,1)} copy(bf16[3,4,4,8,32,24]{5,3,1,0,2,4:T(8,128)(2,1)} %bitcast.215) | data formatting | bytes 1179648 | tf_op jit(solution)/shard_map/transpose | solution.py:88
  119.3 5.5 reshape_reshape.15
  132.0 6.1 reshape_reshape.16
  142.9 6.3 %reshape.558 = bf16[128,2,1152]{2,1,0:T(2,128)(2,1)} reshape(bf16[128,3,4,8,24]{4,3,2,1,0:T(8,128)(2,1)} %bitcast.217) | data formatting | bytes 1179648
  149.2 10.3 %all-to-all-start.1 = ((bf16[128,2,1152]{2,1,0:T(2,128)(2,1)}), bf16[128,2,1152]{2,1,0:T(2,128)(2,1)S(1)}, u32[]{:S(2)}, u32[]{:S(2)}) async-start(bf16[128,2,1152]{2,1,0:T(2,128)(2,1)} %reshape.558), calls=%async_computation.1 | async-start | bytes 1179648 | tf_op jit(solution)/shard_map/all_to_all | solution.py:132
  162.5 11.4 %all-to-all-done.1 = bf16[128,2,1152]{2,1,0:T(2,128)(2,1)S(1)} async-done(((bf16[128,2,1152]{2,1,0:T(2,128)(2,1)}), bf16[128,2,1152]{2,1,0:T(2,128)(2,1)S(1)}, u32[]{:S(2)}, u32[]{:S(2)}) %all-to-all-start.1) | async-done | bytes 589856 | tf_op jit(solution)/shard_map/all_to_all | solution.py:132
  173.9 5.7 reshape.559
  183.8 41.9 %fusion.81 = f32[8,24]{1,0:T(8,128)S(1)} fusion(bf16[8,24,1536]{2,1,0:T(8,128)(2,1)S(1)} %bitcast.234, s32[1536]{0:T(1024)S(1)} %select_n.128, pred[1536]{0:T(1024)(128)(4,1)S(1)} %eq.35), kind=kOutput, calls=%fused_computation.76 | convolution fusion | flops 936935232 | bytes 598272 | tf_op jit(solution)/shard_map/cx,ck->xk/dot_general | solution.py:134
  226.4 7.4 %psum.112 = f32[]{:T(128)} all-reduce(f32[]{:T(128)} %multiply_reduce_fusion.3), channel_id=1, replica_groups=mesh['band_0'=4,'band_1'=4,'band_2'=2,'lev'=4] {'band_0'}, use_global_device_ids=true, to_apply=%region_4.5 | all-reduce | flops 1 | bytes 8 | tf_op jit(solution)/shard_map/psum | solution.py:22
  235.1 7.0 %psum.113 = f32[]{:T(128)} all-reduce(f32[]{:T(128)} %psum.112), channel_id=1, replica_groups=mesh['band_0'=4,'band_1'=4,'band_2'=2,'lev'=4] {'band_1'}, use_global_device_ids=true, to_apply=%region_5.6 | all-reduce | flops 1 | bytes 8 | tf_op jit(solution)/shard_map/psum | solution.py:22
  242.1 7.7 %psum.114 = f32[]{:T(128)} all-reduce(f32[]{:T(128)} %psum.113), channel_id=1, replica_groups=mesh['band_0'=4,'band_1'=4,'band_2'=2,'lev'=4] {'band_2'}, use_global_device_ids=true, to_apply=%region_6.7 | all-reduce | flops 1 | bytes 8 | tf_op jit(solution)/shard_map/psum | solution.py:22
  249.8 7.4 %psum.115 = f32[]{:T(128)} all-reduce(f32[]{:T(128)} %psum.114), channel_id=1, replica_groups=mesh['band_0'=4,'band_1'=4,'band_2'=2,'lev'=4] {'lev'}, use_global_device_ids=true, to_apply=%region_7.8 | all-reduce | flops 1 | bytes 8 | tf_op jit(solution)/shard_map/psum | solution.py:22
  261.2 6.1 reshape_reshape.17
  272.0 5.7 reshape.560
  277.7 20.0 %all_to_all.20 = bf16[128,2,1152]{2,1,0:T(2,128)(2,1)S(1)} all-to-all(bf16[128,2,1152]{2,1,0:T(2,128)(2,1)S(1)} %reshape.560), channel_id=1, replica_groups=mesh['band_0'=4,'band_1'=4,'band_2'=2,'lev'=4] {'band_0','band_1','band_..., dimensions={0} | all-to-all | bytes 1179648 | tf_op jit(solution)/shard_map/all_to_all | solution.py:132
  297.7 5.7 reshape.561
  307.6 41.9 %fusion.78 = f32[8,24]{1,0:T(8,128)S(1)} fusion(bf16[8,24,1536]{2,1,0:T(8,128)(2,1)S(1)} %bitcast.235, s32[1536]{0:T(1024)S(1)} %select_n.128, pred[1536]{0:T(1024)(128)(4,1)S(1)} %eq.35), kind=kOutput, calls=%fused_computation.75 | convolution fusion | flops 936935232 | bytes 598272 | tf_op jit(solution)/shard_map/cx,ck->xk/dot_general | solution.py:134
  350.2 7.4 %psum.116 = f32[]{:T(128)} all-reduce(f32[]{:T(128)} %multiply_reduce_fusion.2), channel_id=1, replica_groups=mesh['band_0'=4,'band_1'=4,'band_2'=2,'lev'=4] {'band_0'}, use_global_device_ids=true, to_apply=%region_10.11 | all-reduce | flops 1 | bytes 8 | tf_op jit(solution)/shard_map/psum | solution.py:22
  357.6 7.0 %psum.117 = f32[]{:T(128)} all-reduce(f32[]{:T(128)} %psum.116), channel_id=1, replica_groups=mesh['band_0'=4,'band_1'=4,'band_2'=2,'lev'=4] {'band_1'}, use_global_device_ids=true, to_apply=%region_11.12 | all-reduce | flops 1 | bytes 8 | tf_op jit(solution)/shard_map/psum | solution.py:22
  365.3 7.7 %psum.118 = f32[]{:T(128)} all-reduce(f32[]{:T(128)} %psum.117), channel_id=1, replica_groups=mesh['band_0'=4,'band_1'=4,'band_2'=2,'lev'=4] {'band_2'}, use_global_device_ids=true, to_apply=%region_12.13 | all-reduce | flops 1 | bytes 8 | tf_op jit(solution)/shard_map/psum | solution.py:22
  373.0 7.4 %psum.119 = f32[]{:T(128)} all-reduce(f32[]{:T(128)} %psum.118), channel_id=1, replica_groups=mesh['band_0'=4,'band_1'=4,'band_2'=2,'lev'=4] {'lev'}, use_global_device_ids=true, to_apply=%region_13.14 | all-reduce | flops 1 | bytes 8 | tf_op jit(solution)/shard_map/psum | solution.py:22
  384.6 6.1 reshape_reshape.18
  395.5 5.7 reshape.562
  401.1 19.9 %all_to_all.21 = bf16[128,2,1152]{2,1,0:T(2,128)(2,1)S(1)} all-to-all(bf16[128,2,1152]{2,1,0:T(2,128)(2,1)S(1)} %reshape.562), channel_id=1, replica_groups=mesh['band_0'=4,'band_1'=4,'band_2'=2,'lev'=4] {'band_0','band_1','band_..., dimensions={0} | all-to-all | bytes 1179648 | tf_op jit(solution)/shard_map/all_to_all | solution.py:132
  421.1 5.7 reshape.563
  431.0 41.9 %fusion.75 = f32[8,24]{1,0:T(8,128)S(1)} fusion(bf16[8,24,1536]{2,1,0:T(8,128)(2,1)S(1)} %bitcast.236, s32[1536]{0:T(1024)S(1)} %select_n.128, pred[1536]{0:T(1024)(128)(4,1)S(1)} %eq.35), kind=kOutput, calls=%fused_computation.74 | convolution fusion | flops 936935232 | bytes 598272 | tf_op jit(solution)/shard_map/cx,ck->xk/dot_general | solution.py:134
  473.5 7.4 %psum.120 = f32[]{:T(128)} all-reduce(f32[]{:T(128)} %multiply_reduce_fusion.1), channel_id=1, replica_groups=mesh['band_0'=4,'band_1'=4,'band_2'=2,'lev'=4] {'band_0'}, use_global_device_ids=true, to_apply=%region_16.17 | all-reduce | flops 1 | bytes 8 | tf_op jit(solution)/shard_map/psum | solution.py:22
  481.0 7.0 %psum.121 = f32[]{:T(128)} all-reduce(f32[]{:T(128)} %psum.120), channel_id=1, replica_groups=mesh['band_0'=4,'band_1'=4,'band_2'=2,'lev'=4] {'band_1'}, use_global_device_ids=true, to_apply=%region_17.18 | all-reduce | flops 1 | bytes 8 | tf_op jit(solution)/shard_map/psum | solution.py:22
  488.7 7.7 %psum.122 = f32[]{:T(128)} all-reduce(f32[]{:T(128)} %psum.121), channel_id=1, replica_groups=mesh['band_0'=4,'band_1'=4,'band_2'=2,'lev'=4] {'band_2'}, use_global_device_ids=true, to_apply=%region_18.19 | all-reduce | flops 1 | bytes 8 | tf_op jit(solution)/shard_map/psum | solution.py:22
  496.4 7.5 %psum.123 = f32[]{:T(128)} all-reduce(f32[]{:T(128)} %psum.122), channel_id=1, replica_groups=mesh['band_0'=4,'band_1'=4,'band_2'=2,'lev'=4] {'lev'}, use_global_device_ids=true, to_apply=%region_19.20 | all-reduce | flops 1 | bytes 8 | tf_op jit(solution)/shard_map/psum | solution.py:22
  507.8 6.1 reshape_reshape.19
  513.9 4.8 copy.94
  518.7 5.7 reshape.564
  524.4 20.0 %all_to_all.22 = bf16[128,2,1152]{2,1,0:T(2,128)(2,1)S(1)} all-to-all(bf16[128,2,1152]{2,1,0:T(2,128)(2,1)S(1)} %reshape.564), channel_id=1, replica_groups=mesh['band_0'=4,'band_1'=4,'band_2'=2,'lev'=4] {'band_0','band_1','band_..., dimensions={0} | all-to-all | bytes 1179648 | tf_op jit(solution)/shard_map/all_to_all | solution.py:132
  544.4 5.7 reshape.565
  554.4 42.7 %exponential_reduce_fusion = (f32[8,24]{1,0:T(8,128)S(1)}, bf16[8,24,1536]{2,1,0:T(8,128)(2,1)}) fusion(bf16[8,24,1536]{2,1,0:T(8,128)(2,1)S(1)} %bitcast.233, s32[1536]{0:T(1024)S(1)} %select_n.128, pred[1536]{0:T(1024)(128)(4,1)S(1)} %eq.35), kind=kOutput, calls=%fused_computation.77 | convolution fusion | flops 937230144 | bytes 1188096 | tf_op jit(solution)/shard_map/cx,ck->xk/dot_general | solution.py:134
  597.8 7.4 %psum.124 = f32[]{:T(128)} all-reduce(f32[]{:T(128)} %multiply_reduce_fusion), channel_id=1, replica_groups=mesh['band_0'=4,'band_1'=4,'band_2'=2,'lev'=4] {'band_0'}, use_global_device_ids=true, to_apply=%region_22.23 | all-reduce | flops 1 | bytes 8 | tf_op jit(solution)/shard_map/psum | solution.py:22
  605.2 7.0 %psum.125 = f32[]{:T(128)} all-reduce(f32[]{:T(128)} %psum.124), channel_id=1, replica_groups=mesh['band_0'=4,'band_1'=4,'band_2'=2,'lev'=4] {'band_1'}, use_global_device_ids=true, to_apply=%region_23.24 | all-reduce | flops 1 | bytes 8 | tf_op jit(solution)/shard_map/psum | solution.py:22
  612.2 7.7 %psum.126 = f32[]{:T(128)} all-reduce(f32[]{:T(128)} %psum.125), channel_id=1, replica_groups=mesh['band_0'=4,'band_1'=4,'band_2'=2,'lev'=4] {'band_2'}, use_global_device_ids=true, to_apply=%region_24.25 | all-reduce | flops 1 | bytes 8 | tf_op jit(solution)/shard_map/psum | solution.py:22
  619.9 7.4 %psum.127 = f32[]{:T(128)} all-reduce(f32[]{:T(128)} %psum.126), channel_id=1, replica_groups=mesh['band_0'=4,'band_1'=4,'band_2'=2,'lev'=4] {'lev'}, use_global_device_ids=true, to_apply=%region_25.26 | all-reduce | flops 1 | bytes 8 | tf_op jit(solution)/shard_map/psum | solution.py:22
  (91 shorter events, 59.5 us)
Async XLA Ops:
  0.6 43.0 %copy-start = (bf16[8,24,1536]{2,1,0:T(8,128)(2,1)S(1)}, bf16[8,24,1536]{2,1,0:T(8,128)(2,1)}, u32[]{:S(2)}) copy-start(bf16[8,24,1536]{2,1,0:T(8,128)(2,1)} %param.15) | copy-start | bytes 1769476
  45.3 23.3 %copy-start.10 = (s32[768]{0:T(1024)S(1)}, s32[768]{0:T(1024)}, u32[]{:S(2)}) copy-start(s32[768]{0:T(1024)} %param.23) | copy-start | bytes 9220
  45.3 23.3 %copy-start.8 = (f32[4]{0:T(128)S(1)}, f32[4]{0:T(128)}, u32[]{:S(2)}) copy-start(f32[4]{0:T(128)} %param.19) | copy-start | bytes 52
  45.4 24.0 %copy-start.9 = (s32[4]{0:T(128)S(1)}, s32[4]{0:T(128)}, u32[]{:S(2)}) copy-start(s32[4]{0:T(128)} %param.21) | copy-start | bytes 52
  56.8 49.6 %all-to-all-start = ((bf16[128,2,1152]{2,1,0:T(2,128)(2,1)}), bf16[128,2,1152]{2,1,0:T(2,128)(2,1)S(1)}, u32[]{:S(2)}, u32[]{:S(2)}) async-start(bf16[128,2,1152]{2,1,0:T(2,128)(2,1)} %reshape.556), calls=%async_computation | async-start | bytes 1179648 | tf_op jit(solution)/shard_map/all_to_all | solution.py:86
  128.4 2.8 copy-start.2
  128.5 2.6 copy-start.6
  149.2 24.6 %all-to-all-start.1 = ((bf16[128,2,1152]{2,1,0:T(2,128)(2,1)}), bf16[128,2,1152]{2,1,0:T(2,128)(2,1)S(1)}, u32[]{:S(2)}, u32[]{:S(2)}) async-start(bf16[128,2,1152]{2,1,0:T(2,128)(2,1)} %reshape.558), calls=%async_computation.1 | async-start | bytes 1179648 | tf_op jit(solution)/shard_map/all_to_all | solution.py:132
  183.8 74.5 %copy-start.7 = (f32[3,2,32,769]{3,2,1,0:T(8,128)S(1)}, f32[3,2,32,769]{3,2,1,0:T(8,128)}, u32[]{:S(2)}) copy-start(f32[3,2,32,769]{3,2,1,0:T(8,128)} %copy-done.6) | copy-start | bytes 1771780
  258.3 2.0 copy-start.3
  381.8 2.0 copy-start.4
  505.0 2.0 copy-start.5
  554.4 74.3 %copy-start.1 = (bf16[8,24,1536]{2,1,0:T(8,128)(2,1)S(1)}, bf16[8,24,1536]{2,1,0:T(8,128)(2,1)}, u32[]{:S(2)}) copy-start(bf16[8,24,1536]{2,1,0:T(8,128)(2,1)} %param.15) | copy-start | bytes 1769476
where the time goes:
time: 638 us; the launch traced here: 629 us
  matrix products  184 us (29%)
  blocking collectives  178 us (28%)
  local copies, waits for them, and re-layouts  172 us (27%)
  other arithmetic  49.4 us (8%)
  starting transfers between devices  22.1 us (3%)
  between operations  11.7 us (2%)
  waiting for transfers between devices  11.4 us (2%)
    dot_general x4, matrix products, body(): jnp.einsum('cx,ck->xk', rows_back, fourier_tab, preferred_element_type=jn...  168 us
    psum x16, blocking collectives, one_axis_at_a_time(): array = lax.psum(array, axis)  118 us
    unnamed x33, local copies, waits for them, and re-layouts  69.3 us
    all_to_all x3, blocking collectives, body(): lax.all_to_all(outgoing, BAND_LEV, split_axis=0, concat_axis=1, tiled=True)  59.9 us
    dot_general x1, other arithmetic, body(): jnp.einsum('ck,xk->cx', fourier_tab, increment.reshape(lev_dev * lat_dev,...  40.4 us
    another operation x4, local copies, waits for them, and re-layouts, body(): waves_bf.reshape(pair_dev, 4, lev_count, lev_dev, band_count, lat_dev)  24.4 us
    gather x2, local copies, waits for them, and re-layouts, body(): stored = legendre[:, lat_map, :]  21.4 us
    transpose x4, local copies, waits for them, and re-layouts, body(): outgoing.transpose(4, 2, 0, 1, 3, 5)  19 us
  transfers between devices with their start and end apart: 2, of which 1 were waited for; matrix products, arithmetic and copies ran while one was open for 6% of the time, Pallas kernels for 0%

commit v1 on v0

v1 whole, which is shorter than its diff:
```python
import math

import jax
import jax.numpy as jnp
import numpy as np
from jax import lax
from jax.sharding import PartitionSpec as P

NT = 767
NLAT = 768
NLON = 1536
LEV = 32
STEPS = 4
DEN = 64
NPAIR = 384
ALL = ("band", "lev")


def canonical_table():
    a = np.arange(NPAIR)[None, :]
    q = np.arange(2)[:, None]
    m = np.where(q == 0, a, NT - a)
    k = np.arange(NLON)
    t = (m[:, :, None] * k % NLON) * (2.0 * math.pi / NLON)
    tab = np.stack([np.cos(t), -np.sin(t)], axis=1) * math.sqrt(2.0 / NLON)
    return tab.astype(np.float32).astype(jnp.bfloat16)


def lat_weights(lat_rows):
    return jnp.cos(math.pi * ((lat_rows.astype(jnp.float32) + 0.5) / NLAT - 0.5))


def body(increment, background, legendre, coupling, damping, target_mass, numerators, pair_low, lat_map):
    nb, nv = lax.axis_size("band"), lax.axis_size("lev")
    band_id, lev_id = lax.axis_index("band"), lax.axis_index("lev")
    lev_dev, lat_dev, _ = increment.shape
    pair_dev = legendre.shape[0]
    onehot = (pair_low[:, None] == jnp.arange(NPAIR)[None, :]).astype(jnp.bfloat16)
    table = jnp.einsum("pa,qrak->pqrk", onehot, jnp.asarray(canonical_table()))
    table = table.reshape(NPAIR * 4, NLON).astype(jnp.bfloat16)
    local_lats = lax.dynamic_slice_in_dim(lat_map, band_id * lat_dev, lat_dev)
    row_weight = lat_weights(local_lats)
    level_weight = 1.0 + 2.0 * jnp.arange(LEV, dtype=jnp.float32) / (LEV - 1)
    normaliser = jnp.sum(level_weight) * jnp.sum(lat_weights(jnp.arange(NLAT))) * NLON
    own = lax.dynamic_slice_in_dim(pair_low, (band_id * nv + lev_id) * pair_dev, pair_dev)
    cols = jnp.arange(NT + 2)
    second = cols[None, :] >= NT + 1 - own[:, None]
    degree = jnp.where(second, cols[None, :] - 1, own[:, None] + cols[None, :]).astype(jnp.float32)
    perm = (lat_map[:, None] == jnp.arange(NLAT)[None, :]).astype(jnp.bfloat16)
    stored = jnp.einsum("sj,pjc->psc", perm, legendre, preferred_element_type=jnp.float32).astype(jnp.bfloat16)
    fourier = jnp.einsum("ck,xk->cx", table, increment.reshape(lev_dev * lat_dev, NLON), preferred_element_type=jnp.float32)
    fourier = (fourier.reshape(NPAIR, 4, lev_dev, lat_dev) * row_weight).astype(jnp.bfloat16)
    got = lax.all_to_all(fourier, ALL, split_axis=0, concat_axis=0, tiled=True)
    got = got.reshape(nb, nv, pair_dev, 4, lev_dev, lat_dev).transpose(2, 3, 1, 4, 0, 5).reshape(pair_dev, 4 * LEV, NLAT)
    coeffs = jnp.einsum("prj,pjc->prc", got, stored, preferred_element_type=jnp.float32)
    coeffs = coeffs.reshape(pair_dev, 2, 2, LEV, NT + 2) * math.sqrt(2.0 / NLAT)
    sec = second[:, None, None, :]
    incr = jnp.where(sec, coeffs[:, 1], coeffs[:, 0]) * (1.0 / (1.0 + (degree / NT) ** 4))[:, None, None, :]
    shape_term = degree * (degree + 1.0) / (NT * (NT + 1.0))
    spectral = background
    states = []
    for s in range(STEPS):
        coupled = 0.7 * spectral + 0.4 * jnp.einsum("lm,prmc->prlc", coupling[s], spectral, precision=lax.Precision.HIGHEST)
        spectral = coupled / (1.0 + damping[s] * shape_term)[:, None, None, :] + numerators[s].astype(jnp.float32) / DEN * incr
        states.append(spectral.astype(jnp.bfloat16))
    st = jnp.stack(states, axis=1)
    zero = jnp.zeros_like(st)
    sec = sec[:, None]
    split = jnp.stack([jnp.where(sec, zero, st), jnp.where(sec, st, zero)], axis=2)
    waves = jnp.einsum("pxc,pjc->pxj", split.reshape(pair_dev, STEPS * 4 * LEV, NT + 2), stored, preferred_element_type=jnp.float32)
    waves = (waves * math.sqrt(2.0 / NT)).astype(jnp.bfloat16)
    waves = waves.reshape(pair_dev, STEPS, 4, nv, lev_dev, nb, lat_dev).transpose(5, 3, 0, 2, 1, 4, 6)
    back = lax.all_to_all(waves.reshape(nb * nv, pair_dev * 4, STEPS * lev_dev * lat_dev), ALL, split_axis=0, concat_axis=0, tiled=True)
    grid = jnp.einsum("cx,ck->xk", back.reshape(NPAIR * 4, STEPS * lev_dev * lat_dev), table, preferred_element_type=jnp.float32)
    grid = grid.reshape(STEPS, lev_dev, lat_dev, NLON)
    top = jnp.max(grid, axis=(2, 3))
    mass = jnp.sum(jnp.sum(jnp.exp(grid - top[:, :, None, None]), axis=3) * row_weight, axis=2)
    tops = lax.all_gather(top, ALL).reshape(nb, nv, STEPS, lev_dev).transpose(0, 2, 1, 3).reshape(nb, STEPS, LEV)
    masses = lax.all_gather(mass, ALL).reshape(nb, nv, STEPS, lev_dev).transpose(0, 2, 1, 3).reshape(nb, STEPS, LEV)
    to_grid = math.sqrt(2.0 / NT) * float(np.float32(math.sqrt(2.0 / NLON)).astype(jnp.bfloat16))
    delta = jnp.zeros((LEV,), jnp.float32)
    fixes = []
    for s in range(STEPS):
        delta = 0.7 * delta + 0.4 * jnp.dot(coupling[s], delta, precision=lax.Precision.HIGHEST)
        shift = delta * to_grid
        total = jnp.sum(jnp.exp(tops[:, s] + shift) * masses[:, s] * level_weight) / normaliser
        fix = jnp.log(target_mass[0] / total)
        fixes.append(fix)
        if s < STEPS - 1:
            delta = delta + fix * (math.sqrt(NT * NLON) / 2.0)
    mine = lax.dynamic_slice_in_dim(shift, lev_id * lev_dev, lev_dev)
    out = (grid[STEPS - 1] + mine[:, None, None]).astype(jnp.bfloat16)
    return out, jnp.stack(fixes)


def solution(mesh):
    placed = (P("lev", "band", None), P(ALL, None, None, None), P(ALL, None, None), P(), P(), P(), P(), P(), P())
    return jax.shard_map(body, mesh=mesh, in_specs=placed, out_specs=(P("lev", "band", None), P()), check_vma=False)
```

time: 638 us -> 330 us (0.52)
  matrix products: 184 us -> 33 us
  blocking collectives: 178 us -> 110 us
  local copies, waits for them, and re-layouts: 172 us -> 117 us
  other arithmetic: 49.4 us -> 11.7 us
  waiting for transfers between devices: 11.4 us -> 18.5 us
    dot_general x14, matrix products: 184 us -> 33 us  [the longest x1 7.98 us: body(): jnp.einsum('cx,ck->xk', back.reshape(NPAIR * 4, STEPS * lev_dev * lat_dev...]
    psum x16 -> x0, blocking collectives: 118 us -> none  [one_axis_at_a_time(): array = lax.psum(array, axis)]
    all_gather x0 -> x2, blocking collectives: none -> 110 us  [the longest x1 55.9 us: body(): lax.all_gather(top, ALL).reshape(nb, nv, STEPS, lev_dev)]
    all_to_all x3 -> x0, blocking collectives: 59.9 us -> none  [body(): lax.all_to_all(outgoing, BAND_LEV, split_axis=0, concat_axis=1, tiled=True)]
    reshape x4 -> x6, local copies, waits for them, and re-layouts: 16 us -> 74.5 us  [the longest x2 33.3 us: body(): waves.reshape(nb * nv, pair_dev * 4, STEPS * lev_dev * lat_dev)]
    unnamed x33 -> x18, local copies, waits for them, and re-layouts: 69.3 us -> 16.4 us
    dot_general x1 -> x0, other arithmetic: 40.4 us -> none  [body(): jnp.einsum('ck,xk->cx', fourier_tab, increment.reshape(lev_dev * lat_dev,...]
    another operation x10 -> x1, local copies, waits for them, and re-layouts: 30.2 us -> 0.22 us  [body(): jnp.stack([jnp.where(sec, zero, st), jnp.where(sec, st, zero)], axis=2)]
  transfers between devices with their start and end apart: 2 -> 2, of which waited for: 1 -> 2; matrix products, arithmetic and copies ran while one was open for 6% -> 9% of each run, Pallas kernels for 0% -> 0%
where the time goes in v1:
time: 330 us; the launch traced here: 323 us
  local copies, waits for them, and re-layouts  117 us (35%)
  blocking collectives  110 us (33%)
  matrix products  33 us (10%)
  starting transfers between devices  22.1 us (7%)
  waiting for transfers between devices  18.5 us (6%)
  other arithmetic  11.7 us (4%)
  between operations  11 us (3%)
    all_gather x1, blocking collectives, body(): lax.all_gather(top, ALL).reshape(nb, nv, STEPS, lev_dev)  55.9 us
    all_gather x1, blocking collectives, body(): lax.all_gather(mass, ALL).reshape(nb, nv, STEPS, lev_dev)  54.5 us
    reshape x2, local copies, waits for them, and re-layouts, body(): waves.reshape(nb * nv, pair_dev * 4, STEPS * lev_dev * lat_dev)  33.3 us
    reshape x1, local copies, waits for them, and re-layouts, body(): waves.reshape(pair_dev, STEPS, 4, nv, lev_dev, nb, lat_dev)  21.4 us
    all_to_all x1, waiting for transfers between devices, body(): lax.all_to_all(waves.reshape(nb * nv, pair_dev * 4, STEPS * lev_dev * lat...  18.3 us
    unnamed x18, local copies, waits for them, and re-layouts  16.4 us
    all_to_all x1, starting transfers between devices, body(): got = lax.all_to_all(fourier, ALL, split_axis=0, concat_axis=0, tiled=True)  11.8 us
    reshape x1, local copies, waits for them, and re-layouts, body(): table = table.reshape(NPAIR * 4, NLON).astype(jnp.bfloat16)  10.7 us
  transfers between devices with their start and end apart: 2, of which 2 were waited for; matrix products, arithmetic and copies ran while one was open for 9% of the time, Pallas kernels for 0%

profile of v1, /device:TPU:1, one launch (start us, length us, event | category | flops | bytes accessed | tf_op | source)
XLA Modules:
  0.0 323.4 jit_solution(942501233835412209)
XLA Ops:
  0.7 0.9 multiply_cosine_fusion
  1.5 5.3 %fusion.42 = bf16[384,2,2,1536]{3,0,2,1:T(8,128)(2,1)S(1)} fusion(bf16[2,2,384,1536]{3,2,1,0:T(8,128)(2,1)} %constant.99.clone, s32[384]{0:T(512)} %param.17), kind=kOutput, calls=%fused_computation.58 | convolution fusion | flops 1812086784 | bytes 9438720 | tf_op jit(solution)/shard_map/pa,qrak->pqrk/dot_general | solution.py:39
  6.8 2.1 copy-done.2
  9.0 1.7 fusion.11
  10.6 5.1 %copy.52 = bf16[384,4,8,24]{3,2,1,0:T(8,128)(2,1)} copy(bf16[384,4,8,24]{0,3,2,1:T(8,128)(2,1)S(1)} %fusion.11) | data formatting | bytes 1179648 | tf_op jit(solution)/shard_map/convert_element_type | solution.py:52
  15.8 6.4 %reshape.487 = bf16[128,2,1152]{2,1,0:T(2,128)(2,1)} reshape(bf16[384,4,8,24]{3,2,1,0:T(8,128)(2,1)} %copy.52) | data formatting | bytes 1179648
  22.2 11.8 %all-to-all-start = ((bf16[128,2,1152]{2,1,0:T(2,128)(2,1)}), bf16[128,2,1152]{2,1,0:T(2,128)(2,1)S(1)}, u32[]{:S(2)}, u32[]{:S(2)}) async-start(bf16[128,2,1152]{2,1,0:T(2,128)(2,1)} %reshape.487), calls=%async_computation | async-start | bytes 1179648 | tf_op jit(solution)/shard_map/all_to_all | solution.py:53
  34.0 0.8 broadcast_subtract_fusion
  34.7 0.7 fusion.96
  37.9 0.7 fusion.97
  41.1 6.9 %convolution_convert_fusion = bf16[768,3,769]{0,2,1:T(8,128)(2,1)} fusion(bf16[3,768,769]{1,2,0:T(8,128)(2,1)} %param.12, s32[768]{0:T(1024)S(1)} %copy-done.7), kind=kOutput, calls=%fused_computation.7 | convolution fusion | flops 2723809536 | bytes 7090176 | tf_op jit(solution)/shard_map/sj,pjc->psc/dot_general | solution.py:50
  48.0 0.3 all-to-all-done
  48.3 5.7 %reshape.488 = bf16[384,4,8,24]{3,2,1,0:T(8,128)(2,1)} reshape(bf16[128,2,1152]{2,1,0:T(2,128)(2,1)S(1)} %all-to-all-done) | data formatting | bytes 1179648
  54.0 7.3 %copy.53 = bf16[3,4,4,8,32,24]{5,4,3,2,1,0:T(8,128)(2,1)} copy(bf16[3,4,4,8,32,24]{5,3,1,0,2,4:T(8,128)(2,1)} %bitcast.272) | data formatting | bytes 1179648 | tf_op jit(solution)/shard_map/transpose | solution.py:54
  61.3 5.5 %reshape.450 = bf16[3,128,768]{2,1,0:T(8,128)(2,1)S(1)} reshape(bf16[3,4,4,8,32,24]{5,4,3,2,1,0:T(8,128)(2,1)} %copy.53) | data formatting | bytes 1179648 | tf_op jit(solution)/shard_map/reshape | solution.py:54
  66.8 3.1 fusion.8
  69.9 0.4 copy.54
  70.4 0.3 copy-done.4
  70.7 2.2 fusion.18
  73.0 0.8 fusion.21
  73.8 0.8 fusion.24
  74.7 0.8 fusion.29
  75.5 0.4 broadcast_select_fusion.1
  76.0 0.3 pad_maximum_fusion
  76.4 0.2 copy.57
  76.6 1.8 copy-done.3
  78.4 2.9 multiply_convert_fusion
  81.2 21.4 %reshape.452 = bf16[3,4,4,4,8,32,24]{6,5,4,3,2,1,0:T(8,128)(2,1)} reshape(bf16[3,512,768]{2,1,0:T(8,128)(2,1)S(1)} %multiply_convert_fusion) | data formatting | bytes 4718592 | tf_op jit(solution)/shard_map/reshape | solution.py:72
  102.7 12.7 %copy.73 = bf16[32,4,3,4,4,8,24]{6,5,4,3,2,1,0:T(8,128)(2,1)} copy(bf16[32,4,3,4,4,8,24]{6,0,5,1,3,4,2:T(8,128)(2,1)} %bitcast.270) | data formatting | bytes 4718592 | tf_op jit(solution)/shard_map/reshape | solution.py:73
  115.3 20.6 %reshape.486 = bf16[128,12,768]{2,1,0:T(8,128)(2,1)} reshape(bf16[32,4,3,4,4,8,24]{6,5,4,3,2,1,0:T(8,128)(2,1)} %copy.73) | data formatting | bytes 4718592 | tf_op jit(solution)/shard_map/reshape | solution.py:73
  136.0 10.3 %all-to-all-start.1 = ((bf16[128,12,768]{2,1,0:T(8,128)(2,1)}), bf16[128,12,768]{2,1,0:T(8,128)(2,1)}, u32[]{:S(2)}, u32[]{:S(2)}) async-start(bf16[128,12,768]{2,1,0:T(8,128)(2,1)} %reshape.486), calls=%async_computation.1 | async-start | bytes 6291456 | tf_op jit(solution)/shard_map/all_to_all | solution.py:73
  146.3 9.4 %copy.61 = bf16[384,2,2,1536]{3,2,1,0:T(2,128)(2,1)} copy(bf16[384,2,2,1536]{3,0,2,1:T(8,128)(2,1)} %copy-done.2) | data formatting | bytes 9437184 | tf_op jit(solution)/shard_map/pa,qrak->pqrk/dot_general | solution.py:39
  155.7 10.7 %reshape.455 = bf16[1536,1536]{1,0:T(8,128)(2,1)} reshape(bf16[384,2,2,1536]{3,2,1,0:T(2,128)(2,1)} %copy.61) | data formatting | bytes 9437184 | tf_op jit(solution)/shard_map/reshape | solution.py:40
  167.0 0.6 fusion.93
  167.6 0.6 cosine_reduce_fusion
  169.6 18.3 %all-to-all-done.1 = bf16[128,12,768]{2,1,0:T(8,128)(2,1)} async-done(((bf16[128,12,768]{2,1,0:T(8,128)(2,1)}), bf16[128,12,768]{2,1,0:T(8,128)(2,1)}, u32[]{:S(2)}, u32[]{:S(2)}) %all-to-all-start.1) | async-done | bytes 2359328 | tf_op jit(solution)/shard_map/all_to_all | solution.py:73
  187.8 3.6 %reshape.454 = bf16[1536,768]{1,0:T(8,128)(2,1)S(1)} reshape(bf16[128,12,768]{2,1,0:T(8,128)(2,1)} %all-to-all-done.1) | data formatting | bytes 4718592 | tf_op jit(solution)/shard_map/reshape | solution.py:74
  191.4 8.0 %fusion.98 = (f32[768]{0:T(1024)S(1)}, f32[768,1536]{1,0:T(8,128)}) fusion(bf16[1536,768]{1,0:T(8,128)(2,1)S(1)} %reshape.454, bf16[1536,1536]{1,0:T(8,128)(2,1)} %reshape.455), kind=kOutput, calls=%fused_computation.142 | convolution fusion | flops 3625057536 | bytes 11799552 | tf_op jit(solution)/shard_map/cx,ck->xk/dot_general | solution.py:74
  199.8 1.3 slice.99
  201.1 3.2 exponential_reduce_fusion
  204.5 54.5 %all-gather.3 = f32[128,4,8]{2,1,0:T(4,128)S(1)} all-gather(f32[1,4,8]{2,1,0:T(4,128)S(1)} %bitcast.287), channel_id=3, replica_groups=mesh['band'=32,'lev'=4] {'band','lev'}, dimensions={0}, use_global_device_ids=true | all-gather | bytes 16512 | tf_op jit(solution)/shard_map/all_gather | solution.py:79
  259.1 55.9 %all-gather.2 = f32[128,4,8]{2,1,0:T(4,128)S(1)} all-gather(f32[1,4,8]{2,1,0:T(4,128)S(1)} %bitcast.286), channel_id=2, replica_groups=mesh['band'=32,'lev'=4] {'band','lev'}, dimensions={0}, use_global_device_ids=true | all-gather | bytes 16512 | tf_op jit(solution)/shard_map/all_gather | solution.py:78
  315.1 0.7 fusion.62
  316.7 0.7 fusion.57
  318.3 0.7 fusion.52
  319.9 0.7 fusion.47
  321.4 1.0 add_convert_fusion
  322.3 0.6 pad_maximum_fusion.2
  (35 shorter events, 1.8 us)
Async XLA Ops:
  0.6 8.3 %copy-start = (bf16[8,24,1536]{2,1,0:T(8,128)(2,1)S(1)}, bf16[8,24,1536]{2,1,0:T(8,128)(2,1)}, u32[]{:S(2)}) copy-start(bf16[8,24,1536]{2,1,0:T(8,128)(2,1)} %param.10) | copy-start | bytes 1769476
  6.8 2.1 copy-start.2
  15.8 19.0 %copy-start.5 = (f32[4]{0:T(128)S(1)}, f32[4]{0:T(128)}, u32[]{:S(2)}) copy-start(f32[4]{0:T(128)} %param.14) | copy-start | bytes 52
  15.8 22.2 %copy-start.6 = (s32[4]{0:T(128)S(1)}, s32[4]{0:T(128)}, u32[]{:S(2)}) copy-start(s32[4]{0:T(128)} %param.16) | copy-start | bytes 52
  15.8 25.4 %copy-start.7 = (s32[768]{0:T(1024)S(1)}, s32[768]{0:T(1024)}, u32[]{:S(2)}) copy-start(s32[768]{0:T(1024)} %param.18) | copy-start | bytes 9220
  22.2 26.1 %all-to-all-start = ((bf16[128,2,1152]{2,1,0:T(2,128)(2,1)}), bf16[128,2,1152]{2,1,0:T(2,128)(2,1)S(1)}, u32[]{:S(2)}, u32[]{:S(2)}) async-start(bf16[128,2,1152]{2,1,0:T(2,128)(2,1)} %reshape.487), calls=%async_computation | async-start | bytes 1179648 | tf_op jit(solution)/shard_map/all_to_all | solution.py:53
  69.9 0.8 copy-start.4
  76.3 2.0 copy-start.3
  136.0 51.8 %all-to-all-start.1 = ((bf16[128,12,768]{2,1,0:T(8,128)(2,1)}), bf16[128,12,768]{2,1,0:T(8,128)(2,1)}, u32[]{:S(2)}, u32[]{:S(2)}) async-start(bf16[128,12,768]{2,1,0:T(8,128)(2,1)} %reshape.486), calls=%async_computation.1 | async-start | bytes 6291456 | tf_op jit(solution)/shard_map/all_to_all | solution.py:73
  201.1 121.8 %copy-start.1 = (bf16[8,24,1536]{2,1,0:T(8,128)(2,1)S(1)}, bf16[8,24,1536]{2,1,0:T(8,128)(2,1)}, u32[]{:S(2)}) copy-start(bf16[8,24,1536]{2,1,0:T(8,128)(2,1)} %param.10) | copy-start | bytes 1769476
